TPU v7x, 32 devices: a whole 2x2x4 slice. The times are simulated.
32 devices in a mesh: replica: 4 (over y, core), shard: 8 (over z, x).
Axes of the slice: x: 2, y: 2, z: 4, core: 2. Of those that a mesh axis runs over, the one named last changes fastest.
Arguments:
- inputs: bfloat16 [512, 2048], P('replica'), may hold values from -6 to 6
- gate_pre: bfloat16 [512, 8192], P('replica', 'shard'), may hold values from -8 to 8
- up_pre: bfloat16 [512, 8192], P('replica', 'shard'), may hold values from -6 to 6
- hidden_grad: bfloat16 [512, 8192], P('replica', 'shard'), may hold values from -6 to 6
- segment_ids: int32 [4, 128], P('replica'), may hold values from 0 to 15, never falling along the last dimension, each value on 1 to 32 neighbouring positions
- doc_weight: int32 [4, 16], P('replica'), may hold values from 1 to 12
- w_gate: bfloat16 [2048, 8192], P(None, 'shard'), may hold values from -0.0625 to 0.0625
- master: float32 [2048, 8192], P('replica', 'shard'), may hold values from -6 to 6
- moment: float32 [2048, 8192], P('replica', 'shard'), may hold values from -10 to 10
- second: float32 [2048, 8192], P('replica', 'shard'), may hold values from 0.5 to 20
Outputs:
- input_grad: bfloat16 [512, 2048], P(('replica', 'shard'))
- up_grad: bfloat16 [512, 8192], P('replica', 'shard')
- master_new: float32 [2048, 8192], P('replica', 'shard')
- moment_new: float32 [2048, 8192], P('replica', 'shard')
- second_new: float32 [2048, 8192], P('replica', 'shard')
Inputs may be any that keep to these rules, and one draw needn't show every extreme that they name: `segment_ids`: within each group the documents occupy runs of positions numbered 0 to 15 in order, each at most 32 long.
All inputs are finite; a program needn't handle non-finite values.
Results may differ from a plain program's by a relative error of at most 0.0049.
Values sent between devices are 32-bit elements; how exact they have to be, the bound alone decides.
A program may use at most 64 MiB of HBM per device.

v0:
```python
import jax
import jax.numpy as jnp
from jax import lax
from jax.sharding import PartitionSpec as P


def token_weights(segment_ids, doc_weight):
    labels = jnp.arange(doc_weight.shape[1], dtype=jnp.int32)
    onehot = segment_ids[:, :, None] == labels[None, None, :]
    return jnp.sum(jnp.where(onehot, doc_weight[:, None, :], 0), axis=2)


def on_device(
    inputs, gate_pre, up_pre, hidden_grad, segment_ids, doc_weight, w_gate, master, moment, second
):
    group_rows = inputs.shape[0]
    replicas = lax.axis_size("replica")
    weights = token_weights(segment_ids, doc_weight)[0]
    local_count = jnp.sum(weights)
    gate_f = gate_pre.astype(jnp.float32)
    sigmoid_gate = jax.nn.sigmoid(gate_f)
    weighted = hidden_grad.astype(jnp.float32) * weights.astype(jnp.float32)[:, None]
    gate_raw = (
        weighted * up_pre.astype(jnp.float32) * sigmoid_gate * (1.0 + gate_f * (1.0 - sigmoid_gate))
    ).astype(jnp.bfloat16)
    up_part = weighted * gate_f * sigmoid_gate
    input_part = lax.dot_general(
        gate_raw, w_gate, (((1,), (1,)), ((), ())), preferred_element_type=jnp.float32
    )
    input_summed = lax.psum_scatter(input_part, "shard", scatter_dimension=0, tiled=True)
    total = lax.psum(local_count, "replica").astype(jnp.float32)
    summed_grad = lax.psum_scatter(
        lax.dot_general(
            inputs, gate_raw, (((0,), (0,)), ((), ())), preferred_element_type=jnp.float32
        ),
        "replica",
        scatter_dimension=0,
        tiled=True,
    )
    summed_grad, total = (summed_grad, total)
    scale = jnp.float32(group_rows * replicas) / total
    group_scale = jnp.float32(group_rows) / total
    input_grad = (input_summed * scale).astype(jnp.bfloat16)
    up_grad = (up_part * scale).astype(jnp.bfloat16)
    grad = summed_grad * group_scale
    moment_new = 0.9 * moment + 0.1 * grad
    second_new = 0.95 * second + 0.05 * grad * grad
    first_fix = moment_new / (1.0 - 0.9**8)
    second_fix = second_new / (1.0 - 0.95**8)
    master_new = master - 0.003 * (first_fix / (jnp.sqrt(second_fix) + 1e-08) + 0.1 * master)
    return (input_grad, up_grad, master_new, moment_new, second_new)


def solution(mesh):
    in_specs = (
        P("replica", None),
        P("replica", "shard"),
        P("replica", "shard"),
        P("replica", "shard"),
        P("replica", None),
        P("replica", None),
        P(None, "shard"),
        P("replica", "shard"),
        P("replica", "shard"),
        P("replica", "shard"),
    )
    out_specs = (
        P(("replica", "shard"), None),
        P("replica", "shard"),
        P("replica", "shard"),
        P("replica", "shard"),
        P("replica", "shard"),
    )
    return jax.shard_map(
        on_device, mesh=mesh, in_specs=in_specs, out_specs=out_specs, check_vma=False
    )
```

profile of v0, /device:TPU:0, one launch (start us, length us, event | category | flops | bytes accessed | tf_op | source)
XLA Modules:
  0.0 174.9 jit_solution(729488284775862574)
XLA Ops:
  7.2 0.0 copy-start
  7.2 0.0 reduce-scatter.3.cloned.1.call-start
  7.2 1.4 select_reduce_fusion
  8.7 0.0 copy-start.2
  8.7 0.0 copy-start.3
  8.7 0.0 copy-start.4
  8.7 5.1 %fusion.11 = f32[128,2048]{1,0:T(8,128)} fusion(bf16[2048,1024]{1,0:T(8,128)(2,1)} %param.16, bf16[128,1024]{1,0:T(8,128)(2,1)} %param.11, bf16[128,1024]{1,0:T(8,128)(2,1)} %param.12, bf16[128,1024]{1,0:T(8,128)(2,1)} %param.13, f32[128]{0:T(128)S(1)} %convert_element_type.29), kind=kOutput, calls=%fused_computation.22 | convolution fusion | flops 538705920 | bytes 6029824 | tf_op jit(solution)/shard_map/dot_general | solution.py:27
  13.8 0.0 reduce-scatter.3.cloned.1.call-update
  13.8 0.0 reduce-scatter.5.cloned.1.call-start
  13.8 0.0 copy-done
  13.9 0.0 copy-done.2
  13.9 0.0 copy-done.3
  13.9 0.0 copy-done.4
  13.9 4.7 %convolution_bitcast_fusion = f32[2048,1024]{0,1:T(8,128)} fusion(bf16[128,2048]{1,0:T(8,128)(2,1)S(1)} %copy-done, bf16[128,1024]{1,0:T(8,128)(2,1)S(1)} %copy-done.2, bf16[128,1024]{1,0:T(8,128)(2,1)S(1)} %copy-done.4, bf16[128,1024]{1,0:T(8,128)(2,1)S(1)} %copy-done.3, f32[128]{0:T(128)S(1)} %convert_element_type.29), kind=kOutput, calls=%fused_computation | convolution fusion | flops 538705920 | bytes 9699840 | tf_op jit(solution)/shard_map/dot_general | solution.py:33
  18.6 0.0 reduce-scatter.5.cloned.1.call-update
  18.6 7.1 %psum.7 = s32[]{:T(128)} all-reduce(s32[]{:T(128)} %get-tuple-element.15), channel_id=1, replica_groups=mesh['replica'=4,'shard'=8] {'replica'}, use_global_device_ids=true, to_apply=%region_3.4 | all-reduce | flops 1 | bytes 8 | tf_op jit(solution)/shard_map/psum | solution.py:31
  26.3 1.9 %copy.22 = f32[512,1024]{0,1:T(8,128)S(1)} copy(f32[512,1024]{1,0:T(8,128)} %param.18) | data formatting | bytes 4194304 | tf_op args[8]
  28.2 2.9 %copy.23 = f32[512,1024]{0,1:T(8,128)} copy(f32[512,1024]{1,0:T(8,128)} %param.19) | data formatting | bytes 4194304 | tf_op args[9]
  31.1 2.9 %copy.25 = f32[512,1024]{0,1:T(8,128)} copy(f32[512,1024]{1,0:T(8,128)} %param.17) | data formatting | bytes 4194304 | tf_op args[7]
  34.1 0.9 fusion.9
  35.0 45.8 %reduce-scatter.3.cloned.1.call-done = f32[16,2048]{1,0:T(8,128)} async-done(((f32[128,2048]{1,0:T(8,128)}), f32[16,2048]{1,0:T(8,128)}) %reduce-scatter.3.cloned.1.call-update) | async-done | bytes 131088 | tf_op jit(solution)/shard_map/reduce_scatter | solution.py:30
  80.9 1.5 multiply_convert_fusion
  82.4 71.3 %reduce-scatter.5.cloned.1.call-done = f32[512,1024]{0,1:T(8,128)} async-done(((f32[2048,1024]{0,1:T(8,128)}), f32[512,1024]{0,1:T(8,128)}) %reduce-scatter.5.cloned.1.call-update) | async-done | bytes 2097168 | tf_op jit(solution)/shard_map/reduce_scatter | solution.py:32
  153.7 6.7 %multiply_subtract_fusion = (f32[512,1024]{0,1:T(8,128)}, f32[512,1024]{0,1:T(8,128)}, f32[512,1024]{0,1:T(8,128)}) fusion(f32[512,1024]{0,1:T(8,128)} %copy.25, f32[512,1024]{0,1:T(8,128)} %reduce-scatter.5.cloned.1.call-done, f32[]{:T(128)S(6)} %div.26, f32[512,1024]{0,1:T(8,128)S(1)} %copy.22, f32[512,1024]{0,1:T(8,128)} %copy.23), kind=kLoop, calls=%fused_computation.3 | loop fusion | flops 8388608 | bytes 14680068 | tf_op jit(solution)/shard_map/sub | solution.py:50
  160.4 2.9 %copy.26 = f32[512,1024]{1,0:T(8,128)} copy(f32[512,1024]{0,1:T(8,128)} %get-tuple-element.17) | data formatting | bytes 4194304
  163.2 0.0 copy-start.1
  163.3 3.0 %copy.27 = f32[512,1024]{1,0:T(8,128)} copy(f32[512,1024]{0,1:T(8,128)} %get-tuple-element.18) | data formatting | bytes 4194304
  166.3 0.0 copy-done.1
  166.3 1.8 %copy.28 = f32[512,1024]{1,0:T(8,128)} copy(f32[512,1024]{0,1:T(8,128)S(1)} %copy-done.1) | data formatting | bytes 4194304
  (1 shorter events, 0.0 us)
Async XLA Ops:
  7.2 6.7 %copy-start = (bf16[128,2048]{1,0:T(8,128)(2,1)S(1)}, bf16[128,2048]{1,0:T(8,128)(2,1)}, u32[]{:S(2)}) copy-start(bf16[128,2048]{1,0:T(8,128)(2,1)} %param.10) | copy-start | bytes 1572868
  7.2 73.7 %reduce-scatter.3.cloned.1.call-start = ((), (), s32[]{:S(2)}) async-start(), calls=%async_computation.2 | async-start | bytes 1179648 | tf_op jit(solution)/shard_map/reduce_scatter | solution.py:30
  8.7 5.2 %copy-start.2 = (bf16[128,1024]{1,0:T(8,128)(2,1)S(1)}, bf16[128,1024]{1,0:T(8,128)(2,1)}, u32[]{:S(2)}) copy-start(bf16[128,1024]{1,0:T(8,128)(2,1)} %param.11) | copy-start | bytes 786436
  8.7 5.2 %copy-start.3 = (bf16[128,1024]{1,0:T(8,128)(2,1)S(1)}, bf16[128,1024]{1,0:T(8,128)(2,1)}, u32[]{:S(2)}) copy-start(bf16[128,1024]{1,0:T(8,128)(2,1)} %param.13) | copy-start | bytes 786436
  8.7 5.2 %copy-start.4 = (bf16[128,1024]{1,0:T(8,128)(2,1)S(1)}, bf16[128,1024]{1,0:T(8,128)(2,1)}, u32[]{:S(2)}) copy-start(bf16[128,1024]{1,0:T(8,128)(2,1)} %param.12) | copy-start | bytes 786436
  13.8 139.9 %reduce-scatter.5.cloned.1.call-start = ((), (), s32[]{:S(2)}) async-start(), calls=%async_computation.3 | async-start | bytes 10485760 | tf_op jit(solution)/shard_map/reduce_scatter | solution.py:32
  163.2 3.0 %copy-start.1 = (f32[512,1024]{0,1:T(8,128)S(1)}, f32[512,1024]{0,1:T(8,128)}, u32[]{:S(2)}) copy-start(f32[512,1024]{0,1:T(8,128)} %get-tuple-element.19) | copy-start | bytes 6291460
Sparse Core Ops, SparseCore 0:
  13.9 66.8 reduce-scatter.2
  83.4 70.1 reduce-scatter.4
where the time goes:
time: 175 us
  waiting for transfers between devices  117 us (67%)
  local copies, waits for them, and re-layouts  15.4 us (9%)
  between operations  14.8 us (8%)
  other arithmetic  10.6 us (6%)
  matrix products  9.77 us (6%)
  blocking collectives  7.08 us (4%)
    reduce_scatter x1, waiting for transfers between devices, on_device(): lax.psum_scatter(lax.dot_general(inputs, gate_raw, (((0,), (0,)), ((), ()...  71.3 us
    reduce_scatter x1, waiting for transfers between devices, on_device(): lax.psum_scatter(input_part, 'shard', scatter_dimension=0, tiled=True)  45.8 us
    unnamed x16, local copies, waits for them, and re-layouts  15.4 us
    psum x1, blocking collectives, on_device(): total = lax.psum(local_count, 'replica').astype(jnp.float32)  7.08 us
    sub x1, other arithmetic, on_device(): master - 0.003 * (first_fix / (jnp.sqrt(second_fix) + 1e-08) + 0.1 * master)  6.7 us
    dot_general x1, matrix products, on_device(): lax.dot_general(gate_raw, w_gate, (((1,), (1,)), ((), ())), preferred_ele...  5.1 us
    dot_general x1, matrix products, on_device(): lax.dot_general(inputs, gate_raw, (((0,), (0,)), ((), ())), preferred_ele...  4.67 us
  transfers between devices with their start and end apart: 2, of which 2 were waited for; matrix products, arithmetic and copies ran while one was open for 8% of the time, Pallas kernels for 0%

commit v1 on v0

--- a/solution.py
+++ b/solution.py
@@ -1,7 +1,14 @@
+import functools
+
 import jax
 import jax.numpy as jnp
 from jax import lax
+from jax.experimental import pallas as pl
+from jax.experimental.pallas import tpu as pltpu
 from jax.sharding import PartitionSpec as P
+
+MESH = pl.DeviceIdType.MESH
+QUARTERS = 4
 
 
 def token_weights(segment_ids, doc_weight):
@@ -10,7 +17,16 @@
     return jnp.sum(jnp.where(onehot, doc_weight[:, None, :], 0), axis=2)
 
 
-def on_device(
+def adamw(grad, master, moment, second):
+    moment_new = 0.9 * moment + 0.1 * grad
+    second_new = 0.95 * second + 0.05 * grad * grad
+    first_fix = moment_new / (1.0 - 0.9**8)
+    second_fix = second_new / (1.0 - 0.95**8)
+    master_new = master - 0.003 * (first_fix / (jnp.sqrt(second_fix) + 1e-08) + 0.1 * master)
+    return master_new, moment_new, second_new
+
+
+def reduce_path(
     inputs, gate_pre, up_pre, hidden_grad, segment_ids, doc_weight, w_gate, master, moment, second
 ):
     group_rows = inputs.shape[0]
@@ -37,18 +53,280 @@
         scatter_dimension=0,
         tiled=True,
     )
-    summed_grad, total = (summed_grad, total)
     scale = jnp.float32(group_rows * replicas) / total
     group_scale = jnp.float32(group_rows) / total
     input_grad = (input_summed * scale).astype(jnp.bfloat16)
     up_grad = (up_part * scale).astype(jnp.bfloat16)
-    grad = summed_grad * group_scale
-    moment_new = 0.9 * moment + 0.1 * grad
-    second_new = 0.95 * second + 0.05 * grad * grad
-    first_fix = moment_new / (1.0 - 0.9**8)
-    second_fix = second_new / (1.0 - 0.95**8)
-    master_new = master - 0.003 * (first_fix / (jnp.sqrt(second_fix) + 1e-08) + 0.1 * master)
-    return (input_grad, up_grad, master_new, moment_new, second_new)
+    return (input_grad, up_grad) + adamw(summed_grad * group_scale, master, moment, second)
+
+
+def flip(index, bit):
+    return index + bit - 2 * bit * lax.rem(lax.div(index, bit), 2)
+
+
+def exchange_kernel(
+    x_hbm, gate_hbm, up_hbm, hid_hbm, seg_hbm, dw_hbm, w_hbm,
+    xo_ref, go_ref, sum_ref, upo_ref, tot_ref,
+    x_v, gate_v, up_v, hid_v, seg_ref, dw_ref, w_v, x32, g32, part, cnt,
+    xp, xq, gr, rs1, rs2, rs3, cntr, lsem, ssem, rsem,
+):
+    r, s = lax.axis_index("replica"), lax.axis_index("shard")
+    core, side, across = flip(r, 1), flip(r, 2), flip(flip(r, 1), 2)
+    near, mid, far = flip(s, 1), flip(s, 2), flip(s, 4)
+    rows, width = x_v.shape[0], xo_ref.shape[1]
+    quarter = rows // QUARTERS
+    tall = sum_ref.shape[0]
+    f32, bf16 = jnp.float32, jnp.bfloat16
+
+    local = []
+    for k, (src, dst) in enumerate(
+        [
+            (x_hbm, x_v), (seg_hbm, seg_ref), (dw_hbm, dw_ref), (gate_hbm, gate_v),
+            (hid_hbm, hid_v), (up_hbm, up_v), (w_hbm, w_v),
+        ]
+    ):
+        copy = pltpu.make_async_copy(src, dst, lsem.at[k])
+        copy.start()
+        local.append(copy)
+
+    barrier = pltpu.get_barrier_semaphore()
+    peers = [(core, s), (side, s), (across, s), (r, near), (r, mid), (r, far)]
+    for peer in peers:
+        pl.semaphore_signal(barrier, inc=1, device_id=peer, device_id_type=MESH)
+
+    started = []
+
+    def push(src, dst, peer):
+        k = len(started)
+        copy = pltpu.make_async_remote_copy(
+            src_ref=src, dst_ref=dst, send_sem=ssem.at[k], recv_sem=rsem.at[k],
+            device_id=peer, device_id_type=MESH,
+        )
+        copy.start()
+        started.append(copy)
+        return copy
+
+    local[0].wait()
+    x32[...] = x_v[...].astype(f32)
+    own = pl.ds(pl.multiple_of(r * width, width), width)
+    xo_ref[pl.ds(0, rows), :] = x_v[:, own]
+
+    local[1].wait()
+    local[2].wait()
+    docs = dw_ref.shape[1]
+    seg = jnp.broadcast_to(seg_ref[...].astype(f32), (128, rows)).T[:, :docs]
+    labels = lax.broadcasted_iota(jnp.int32, (rows, docs), 1).astype(f32)
+    dw = jnp.broadcast_to(dw_ref[...].astype(f32), (rows, docs))
+    tw = jnp.sum(jnp.where(seg == labels, dw, 0.0), axis=1, keepdims=True)
+    count = jnp.sum(tw, axis=0, keepdims=True)
+    cnt[...] = jnp.broadcast_to(count, cnt.shape)
+
+    pl.semaphore_wait(barrier, len(peers))
+
+    q = lax.rem(s, QUARTERS)
+
+    def at_quarter(index):
+        return pl.ds(pl.multiple_of(index * quarter, quarter), quarter)
+
+    def columns(owner):
+        return pl.ds(pl.multiple_of(owner * width, width), width)
+
+    x_side = push(x32.at[at_quarter(q), columns(side)], xq.at[0, 0], (side, s))
+    x_across = push(x32.at[at_quarter(q), columns(across)], xq.at[1, 0], (across, s))
+    x_core = push(x32.at[:, columns(core)], xp, (core, s))
+    counts = [push(cnt, cntr.at[k], (peer, s)) for k, peer in enumerate((core, side, across))]
+
+    for k in (3, 4, 5):
+        local[k].wait()
+    for k in range(QUARTERS):
+        at = pl.ds(k * quarter, quarter)
+        g = gate_v[at, :].astype(f32)
+        sig = jax.nn.sigmoid(g)
+        h = hid_v[at, :].astype(f32) * tw[k * quarter : (k + 1) * quarter, :]
+        raw = (h * up_v[at, :].astype(f32) * sig * (1.0 + g * (1.0 - sig))).astype(bf16)
+        upo_ref[at, :] = h * g * sig
+        go_ref[at, :] = raw
+        g32[at, :] = raw.astype(f32)
+
+    g_side = [
+        push(g32.at[pl.ds(k * quarter, quarter), :], gr.at[1, pl.ds(k * quarter, quarter), :], (side, s))
+        for k in range(QUARTERS)
+    ]
+    g_core = push(g32, gr.at[0], (core, s))
+
+    local[6].wait()
+    step = w_v.shape[0] // QUARTERS
+    for k in range(QUARTERS):
+        part[:, pl.ds(k * step, step)] = lax.dot_general(
+            go_ref[pl.ds(0, rows), :], w_v[pl.ds(k * step, step), :],
+            (((1,), (1,)), ((), ())), preferred_element_type=f32,
+        )
+
+    def block(index):
+        return pl.ds(pl.multiple_of(index * tall, tall), tall)
+
+    first = {}
+    for slot, (delta, index) in enumerate(
+        [(6, flip(flip(near, 2), 4)), (2, flip(near, 2)), (4, flip(near, 4)), (0, near)]
+    ):
+        first[delta] = (slot, push(part.at[block(index), :], rs1.at[slot], (r, near)))
+
+    def absorb(delta, index):
+        slot, copy = first[delta]
+        copy.wait_recv()
+        part[block(index), :] = part[block(index), :] + rs1[slot]
+
+    def keep_x(group, slot, index):
+        xo_ref[pl.ds(pl.multiple_of((group + 2) * rows + index * quarter, quarter), quarter), :] = (
+            xq[group, slot].astype(bf16)
+        )
+
+    def keep_g(group, k):
+        at = pl.ds(k * quarter, quarter)
+        go_ref[pl.ds((group + 1) * rows + k * quarter, quarter), :] = gr[group, at, :].astype(bf16)
+
+    def relay_g(k):
+        at = pl.ds(k * quarter, quarter)
+        g_side[k].wait_recv()
+        copy = push(gr.at[1, at, :], gr.at[2, at, :], (core, s))
+        keep_g(1, k)
+        return copy
+
+    x_near, x_mid = [], []
+    for group, copy in enumerate((x_side, x_across)):
+        copy.wait_recv()
+        x_near.append(push(xq.at[group, 0], xq.at[group, 1], (r, near)))
+        x_mid.append(push(xq.at[group, 0], xq.at[group, 2], (r, mid)))
+    x_core.wait_recv()
+    xo_ref[pl.ds(rows, rows), :] = xp[...].astype(bf16)
+    g_core.wait_recv()
+    for k in range(QUARTERS):
+        keep_g(0, k)
+    for group in range(2):
+        keep_x(group, 0, q)
+    for copy in counts:
+        copy.wait_recv()
+    tot_ref[...] = cnt[...] + cntr[0] + cntr[1] + cntr[2]
+
+    g_across = [relay_g(0)]
+    absorb(6, flip(mid, 4))
+    second_far = push(part.at[block(flip(mid, 4)), :], rs2.at[0], (r, mid))
+    absorb(2, mid)
+    second_own = push(part.at[block(mid), :], rs2.at[1], (r, mid))
+    g_across.append(relay_g(1))
+    absorb(4, far)
+    second_far.wait_recv()
+    part[block(far), :] = part[block(far), :] + rs2[0]
+    third = push(part.at[block(far), :], rs3, (r, far))
+    x_last = []
+    for group in range(2):
+        x_near[group].wait_recv()
+        x_last.append(push(xq.at[group, 1], xq.at[group, 3], (r, mid)))
+        keep_x(group, 1, lax.rem(near, QUARTERS))
+    g_across.append(relay_g(2))
+    for group in range(2):
+        x_mid[group].wait_recv()
+        keep_x(group, 2, lax.rem(mid, QUARTERS))
+    for k in range(2):
+        g_across[k].wait_recv()
+        keep_g(2, k)
+    absorb(0, s)
+    second_own.wait_recv()
+    g_across.append(relay_g(3))
+    for group in range(2):
+        x_last[group].wait_recv()
+        keep_x(group, 3, lax.rem(flip(near, 2), QUARTERS))
+    third.wait_recv()
+    sum_ref[...] = part[block(s), :] + rs2[1] + rs3[...]
+    for k in range(2, QUARTERS):
+        g_across[k].wait_recv()
+        keep_g(2, k)
+    for copy in started:
+        copy.wait_send()
+
+
+def exchange(inputs, gate_pre, up_pre, hidden_grad, segment_ids, doc_weight, w_gate):
+    replicas, shards = lax.axis_size("replica"), lax.axis_size("shard")
+    rows, features = inputs.shape
+    hidden = gate_pre.shape[1]
+    width, tall, quarter = features // replicas, rows // shards, rows // QUARTERS
+    f32, bf16 = jnp.float32, jnp.bfloat16
+    vmem = pl.BlockSpec(memory_space=pltpu.VMEM)
+    hbm = pl.BlockSpec(memory_space=pltpu.HBM)
+    copies = 30
+    return pl.pallas_call(
+        exchange_kernel,
+        out_shape=(
+            jax.ShapeDtypeStruct((replicas * rows, width), bf16),
+            jax.ShapeDtypeStruct((replicas * rows, hidden), bf16),
+            jax.ShapeDtypeStruct((tall, features), f32),
+            jax.ShapeDtypeStruct((rows, hidden), f32),
+            jax.ShapeDtypeStruct((8, 128), f32),
+        ),
+        in_specs=[hbm] * 7,
+        out_specs=(vmem,) * 5,
+        scratch_shapes=[
+            pltpu.VMEM((rows, features), bf16),
+            pltpu.VMEM((rows, hidden), bf16),
+            pltpu.VMEM((rows, hidden), bf16),
+            pltpu.VMEM((rows, hidden), bf16),
+            pltpu.VMEM(segment_ids.shape, jnp.int32),
+            pltpu.VMEM(doc_weight.shape, jnp.int32),
+            pltpu.VMEM((features, hidden), bf16),
+            pltpu.VMEM((rows, features), f32),
+            pltpu.VMEM((rows, hidden), f32),
+            pltpu.VMEM((rows, features), f32),
+            pltpu.VMEM((8, 128), f32),
+            pltpu.VMEM((rows, width), f32),
+            pltpu.VMEM((2, QUARTERS, quarter, width), f32),
+            pltpu.VMEM((3, rows, hidden), f32),
+            pltpu.VMEM((4, tall, features), f32),
+            pltpu.VMEM((2, tall, features), f32),
+            pltpu.VMEM((tall, features), f32),
+            pltpu.VMEM((3, 8, 128), f32),
+            pltpu.SemaphoreType.DMA((7,)),
+            pltpu.SemaphoreType.DMA((copies,)),
+            pltpu.SemaphoreType.DMA((copies,)),
+        ],
+        compiler_params=pltpu.CompilerParams(
+            collective_id=0, has_side_effects=True, vmem_limit_bytes=24 * 1024 * 1024
+        ),
+        cost_estimate=pl.CostEstimate(
+            flops=2 * rows * hidden * features, bytes_accessed=40 * 1024 * 1024, transcendentals=0
+        ),
+        name="exchange",
+    )(inputs, gate_pre, up_pre, hidden_grad, segment_ids, doc_weight, w_gate)
+
+
+def gather_path(
+    inputs, gate_pre, up_pre, hidden_grad, segment_ids, doc_weight, w_gate, master, moment, second
+):
+    group_rows = inputs.shape[0]
+    replicas = lax.axis_size("replica")
+    x_all, gate_all, input_summed, up_part, totals = exchange(
+        inputs, gate_pre, up_pre, hidden_grad, segment_ids, doc_weight, w_gate
+    )
+    total = totals[0, 0]
+    scale = jnp.float32(group_rows * replicas) / total
+    group_scale = jnp.float32(group_rows) / total
+    input_grad = (input_summed * scale).astype(jnp.bfloat16)
+    up_grad = (up_part * scale).astype(jnp.bfloat16)
+    summed_grad = lax.dot_general(
+        x_all, gate_all, (((0,), (0,)), ((), ())), preferred_element_type=jnp.float32
+    )
+    return (input_grad, up_grad) + adamw(summed_grad * group_scale, master, moment, second)
+
+
+def on_device(*args):
+    inputs, gate_pre = args[:2]
+    replicas, shards = lax.axis_size("replica"), lax.axis_size("shard")
+    rows, features = inputs.shape
+    hidden = gate_pre.shape[1]
+    gathered = replicas * rows * (features // replicas + hidden)
+    fits = rows % (QUARTERS * 32) == 0 and features % (replicas * 128) == 0
+    if (replicas, shards) == (4, 8) and fits and gathered <= features * hidden:
+        return gather_path(*args)
+    return reduce_path(*args)
 
 
 def solution(mesh):

time: 175 us -> 44.1 us (0.25)
  waiting for transfers between devices: 117 us -> 0 us
  Pallas kernels: 0 us -> 27.5 us
  between operations: 14.8 us -> 2.04 us
  other arithmetic: 10.6 us -> 1.38 us
  local copies, waits for them, and re-layouts: 15.4 us -> 7.9 us
  blocking collectives: 7.08 us -> 0 us
  matrix products: 9.77 us -> 4.9 us
    reduce_scatter x2 -> x0, waiting for transfers between devices: 117 us -> none  [the longest x1 71.3 us: on_device(): lax.psum_scatter(lax.dot_general(inputs, gate_raw, (((0,), (0,)), ((), ()...]
    pallas_call x0 -> x1, Pallas kernels: none -> 27.5 us  [exchange(): pl.pallas_call(exchange_kernel, out_shape=(jax.ShapeDtypeStruct((replicas...]
    unnamed x16 -> x20, local copies, waits for them, and re-layouts: 15.4 us -> 7.39 us
    psum x1 -> x0, blocking collectives: 7.08 us -> none  [on_device(): total = lax.psum(local_count, 'replica').astype(jnp.float32)]
    sub x1 -> x0, other arithmetic: 6.7 us -> none  [on_device(): master - 0.003 * (first_fix / (jnp.sqrt(second_fix) + 1e-08) + 0.1 * master)]
    dot_general x2 -> x1, matrix products: 9.77 us -> 4.9 us  [gather_path(): lax.dot_general(x_all, gate_all, (((0,), (0,)), ((), ())), preferred_elem...]
  transfers between devices with their start and end apart: 2 -> 0, of which waited for: 2 -> 0; matrix products, arithmetic and copies ran while one was open for 8% -> 0% of each run, Pallas kernels for 0% -> 0%
where the time goes in v1:
time: 44.1 us; the launch traced here: 43.8 us
  Pallas kernels  27.5 us (62%)
  local copies, waits for them, and re-layouts  7.9 us (18%)
  matrix products  4.9 us (11%)
  between operations  2.04 us (5%)
  other arithmetic  1.38 us (3%)
    pallas_call x1, Pallas kernels, exchange(): pl.pallas_call(exchange_kernel, out_shape=(jax.ShapeDtypeStruct((replicas...  27.5 us
    unnamed x20, local copies, waits for them, and re-layouts  7.39 us
    dot_general x1, matrix products, gather_path(): lax.dot_general(x_all, gate_all, (((0,), (0,)), ((), ())), preferred_elem...  4.9 us

profile of v1, /device:TPU:0, one launch (start us, length us, event | category | flops | bytes accessed | tf_op | source)
XLA Modules:
  0.0 43.8 jit_solution(2469886138450866647)
XLA Ops:
  0.6 0.0 copy-start
  0.6 2.2 %copy-done = bf16[2048,1024]{1,0:T(8,128)(2,1)S(1)} copy-done((bf16[2048,1024]{1,0:T(8,128)(2,1)S(1)}, bf16[2048,1024]{1,0:T(8,128)(2,1)}, u32[]{:S(2)}) %copy-start) | copy-done | bytes 4194328
  2.8 0.0 copy-start.1
  2.8 1.0 %copy-done.1 = bf16[128,2048]{1,0:T(8,128)(2,1)S(1)} copy-done((bf16[128,2048]{1,0:T(8,128)(2,1)S(1)}, bf16[128,2048]{1,0:T(8,128)(2,1)}, u32[]{:S(2)}) %copy-start.1) | copy-done | bytes 524312
  3.9 0.0 copy-start.2
  3.9 0.9 %copy-done.2 = bf16[128,1024]{1,0:T(8,128)(2,1)S(1)} copy-done((bf16[128,1024]{1,0:T(8,128)(2,1)S(1)}, bf16[128,1024]{1,0:T(8,128)(2,1)}, u32[]{:S(2)}) %copy-start.2) | copy-done | bytes 262168
  4.8 0.0 copy-start.3
  4.8 0.9 %copy-done.3 = bf16[128,1024]{1,0:T(8,128)(2,1)S(1)} copy-done((bf16[128,1024]{1,0:T(8,128)(2,1)S(1)}, bf16[128,1024]{1,0:T(8,128)(2,1)}, u32[]{:S(2)}) %copy-start.3) | copy-done | bytes 262168
  5.8 0.0 copy-start.4
  5.8 0.9 %copy-done.4 = bf16[128,1024]{1,0:T(8,128)(2,1)S(1)} copy-done((bf16[128,1024]{1,0:T(8,128)(2,1)S(1)}, bf16[128,1024]{1,0:T(8,128)(2,1)}, u32[]{:S(2)}) %copy-start.4) | copy-done | bytes 262168
  6.7 0.0 copy-start.5
  6.7 0.7 %copy-done.5 = s32[1,128]{1,0:T(1,128)S(1)} copy-done((s32[1,128]{1,0:T(1,128)S(1)}, s32[1,128]{1,0:T(1,128)}, u32[]{:S(2)}) %copy-start.5) | copy-done | bytes 536
  7.4 0.0 copy-start.6
  7.4 0.7 %copy-done.6 = s32[1,16]{1,0:T(1,128)S(1)} copy-done((s32[1,16]{1,0:T(1,128)S(1)}, s32[1,16]{1,0:T(1,128)}, u32[]{:S(2)}) %copy-start.6) | copy-done | bytes 88
  8.0 0.0 copy-start.7
  8.0 0.0 copy-start.8
  8.0 0.0 copy-start.9
  8.0 27.5 %exchange.1 = (bf16[512,512]{1,0:T(8,128)(2,1)S(1)}, bf16[512,1024]{1,0:T(8,128)(2,1)S(1)}, f32[16,2048]{1,0:T(8,128)S(1)}, f32[128,1024]{1,0:T(8,128)S(1)}, f32[8,128]{1,0:T(8,128)S(1)}) custom-call(bf16[128,2048]{1,0:T(8,128)(2,1)S(1)} %copy-done.1, bf16[128,1024]{1,0:T(8,128)(2,1)S(1)} %copy-done.2, bf16[128,1024]{1,0:T(8,128)(2,1)S(1)} %copy-done.3, ...), custom_call_target="tpu_custom_call" | custom-call | flops 536870912 | bytes 41943040 | tf_op jit(solution)/shard_map/exchange/pallas_call | solution.py:257
  35.6 0.5 %slice.3 = f32[1,1]{1,0:T(1,128)} slice(f32[8,128]{1,0:T(8,128)S(1)} %get-tuple-element.11), slice={[0:1], [0:1]} | slice | bytes 8 | tf_op jit(solution)/shard_map/slice | solution.py:309
  37.5 0.6 %multiply_convert_fusion.1 = bf16[16,2048]{1,0:T(8,128)(2,1)} fusion(f32[16,2048]{1,0:T(8,128)S(1)} %get-tuple-element.10, f32[]{:T(128)} %bitcast), kind=kLoop, calls=%fused_computation.5 | loop fusion | flops 65536 | bytes 196612 | tf_op jit(solution)/shard_map/convert_element_type | solution.py:312
  38.1 0.7 %multiply_convert_fusion = bf16[128,1024]{1,0:T(8,128)(2,1)} fusion(f32[128,1024]{1,0:T(8,128)S(1)} %get-tuple-element.12, f32[]{:T(128)} %bitcast), kind=kLoop, calls=%fused_computation.4 | loop fusion | flops 262144 | bytes 786436 | tf_op jit(solution)/shard_map/convert_element_type | solution.py:313
  38.8 0.0 copy-done.7
  38.8 0.0 copy-done.8
  38.8 0.0 copy-done.9
  38.9 4.9 %multiply_subtract_fusion = (f32[512,1024]{1,0:T(8,128)}, f32[512,1024]{1,0:T(8,128)}, f32[512,1024]{1,0:T(8,128)}) fusion(f32[512,1024]{1,0:T(8,128)S(1)} %copy-done.7, f32[]{:T(128)} %bitcast.1, f32[512,1024]{1,0:T(8,128)S(1)} %copy-done.8, f32[512,1024]{1,0:T(8,128)S(1)} %copy-done.9, bf16[512,512]{1,0:T(8,128)(2,1)S(1)} %get-tuple-element.13, ...), kind=kOutput, calls=%fused_computation.2 | convolution fusion | flops 545259520 | bytes 14155780 | tf_op jit(solution)/shard_map/dot_general | solution.py:314
Async XLA Ops:
  0.6 2.2 %copy-start = (bf16[2048,1024]{1,0:T(8,128)(2,1)S(1)}, bf16[2048,1024]{1,0:T(8,128)(2,1)}, u32[]{:S(2)}) copy-start(bf16[2048,1024]{1,0:T(8,128)(2,1)} %w_hbm.1) | copy-start | bytes 12582916
  2.8 1.0 %copy-start.1 = (bf16[128,2048]{1,0:T(8,128)(2,1)S(1)}, bf16[128,2048]{1,0:T(8,128)(2,1)}, u32[]{:S(2)}) copy-start(bf16[128,2048]{1,0:T(8,128)(2,1)} %x_hbm.1) | copy-start | bytes 1572868
  3.9 0.9 %copy-start.2 = (bf16[128,1024]{1,0:T(8,128)(2,1)S(1)}, bf16[128,1024]{1,0:T(8,128)(2,1)}, u32[]{:S(2)}) copy-start(bf16[128,1024]{1,0:T(8,128)(2,1)} %gate_hbm.1) | copy-start | bytes 786436
  4.8 0.9 %copy-start.3 = (bf16[128,1024]{1,0:T(8,128)(2,1)S(1)}, bf16[128,1024]{1,0:T(8,128)(2,1)}, u32[]{:S(2)}) copy-start(bf16[128,1024]{1,0:T(8,128)(2,1)} %up_hbm.1) | copy-start | bytes 786436
  5.8 0.9 %copy-start.4 = (bf16[128,1024]{1,0:T(8,128)(2,1)S(1)}, bf16[128,1024]{1,0:T(8,128)(2,1)}, u32[]{:S(2)}) copy-start(bf16[128,1024]{1,0:T(8,128)(2,1)} %hid_hbm.1) | copy-start | bytes 786436
  6.7 0.7 %copy-start.5 = (s32[1,128]{1,0:T(1,128)S(1)}, s32[1,128]{1,0:T(1,128)}, u32[]{:S(2)}) copy-start(s32[1,128]{1,0:T(1,128)} %seg_hbm.1) | copy-start | bytes 1540
  7.4 0.7 %copy-start.6 = (s32[1,16]{1,0:T(1,128)S(1)}, s32[1,16]{1,0:T(1,128)}, u32[]{:S(2)}) copy-start(s32[1,16]{1,0:T(1,128)} %dw_hbm.1) | copy-start | bytes 196
  8.0 30.8 %copy-start.7 = (f32[512,1024]{1,0:T(8,128)S(1)}, f32[512,1024]{1,0:T(8,128)}, u32[]{:S(2)}) copy-start(f32[512,1024]{1,0:T(8,128)} %param.17) | copy-start | bytes 6291460
  8.0 30.8 %copy-start.8 = (f32[512,1024]{1,0:T(8,128)S(1)}, f32[512,1024]{1,0:T(8,128)}, u32[]{:S(2)}) copy-start(f32[512,1024]{1,0:T(8,128)} %param.18) | copy-start | bytes 6291460
  8.0 30.8 %copy-start.9 = (f32[512,1024]{1,0:T(8,128)S(1)}, f32[512,1024]{1,0:T(8,128)}, u32[]{:S(2)}) copy-start(f32[512,1024]{1,0:T(8,128)} %param.19) | copy-start | bytes 6291460

commit v2 on v1

--- a/solution.py
+++ b/solution.py
@@ -66,11 +66,12 @@
 
 def exchange_kernel(
     x_hbm, gate_hbm, up_hbm, hid_hbm, seg_hbm, dw_hbm, w_hbm,
-    xo_ref, go_ref, sum_ref, upo_ref, tot_ref,
-    x_v, gate_v, up_v, hid_v, seg_ref, dw_ref, w_v, x32, g32, part, cnt,
-    xp, xq, gr, rs1, rs2, rs3, cntr, lsem, ssem, rsem,
+    xo_hbm, go_hbm, sum_hbm, upo_hbm, gs_hbm,
+    xo_ref, go_ref, sum_ref, upo_ref, gs_ref, x_v, gate_v, up_v, hid_v, seg_ref, dw_ref, w_v, x32, g32, part, cnt,
+    xp, xq, gr, rs1, rs2, rs3, cntr, lsem, osem, ssem, rsem,
 ):
     r, s = lax.axis_index("replica"), lax.axis_index("shard")
+    replicas = lax.axis_size("replica")
     core, side, across = flip(r, 1), flip(r, 2), flip(flip(r, 1), 2)
     near, mid, far = flip(s, 1), flip(s, 2), flip(s, 4)
     rows, width = x_v.shape[0], xo_ref.shape[1]
@@ -94,7 +95,12 @@
     for peer in peers:
         pl.semaphore_signal(barrier, inc=1, device_id=peer, device_id_type=MESH)
 
-    started = []
+    started, written = [], []
+
+    def write(src, dst):
+        copy = pltpu.make_async_copy(src, dst, osem.at[len(written)])
+        copy.start()
+        written.append(copy)
 
     def push(src, dst, peer):
         k = len(started)
@@ -206,7 +212,14 @@
         keep_x(group, 0, q)
     for copy in counts:
         copy.wait_recv()
-    tot_ref[...] = cnt[...] + cntr[0] + cntr[1] + cntr[2]
+    total = (cnt[...] + cntr[0] + cntr[1] + cntr[2])[0:1, 0:1]
+    scale = f32(rows * replicas) / total
+    gs_ref[...] = jnp.broadcast_to(f32(rows) / total, gs_ref.shape)
+    upo_ref[...] = upo_ref[...] * scale
+    write(xo_ref.at[pl.ds(0, 2 * rows), :], xo_hbm.at[pl.ds(0, 2 * rows), :])
+    write(go_ref.at[pl.ds(0, 2 * rows), :], go_hbm.at[pl.ds(0, 2 * rows), :])
+    write(gs_ref, gs_hbm)
+    write(upo_ref, upo_hbm)
 
     g_across = [relay_g(0)]
     absorb(6, flip(mid, 4))
@@ -236,13 +249,19 @@
     for group in range(2):
         x_last[group].wait_recv()
         keep_x(group, 3, lax.rem(flip(near, 2), QUARTERS))
+    write(xo_ref.at[pl.ds(2 * rows, 2 * rows), :], xo_hbm.at[pl.ds(2 * rows, 2 * rows), :])
+    write(go_ref.at[pl.ds(2 * rows, rows), :], go_hbm.at[pl.ds(2 * rows, rows), :])
     third.wait_recv()
-    sum_ref[...] = part[block(s), :] + rs2[1] + rs3[...]
+    sum_ref[...] = (part[block(s), :] + rs2[1] + rs3[...]) * scale
+    write(sum_ref, sum_hbm)
     for k in range(2, QUARTERS):
         g_across[k].wait_recv()
         keep_g(2, k)
+    write(go_ref.at[pl.ds(3 * rows, rows), :], go_hbm.at[pl.ds(3 * rows, rows), :])
     for copy in started:
         copy.wait_send()
+    for copy in written:
+        copy.wait()
 
 
 def exchange(inputs, gate_pre, up_pre, hidden_grad, segment_ids, doc_weight, w_gate):
@@ -251,7 +270,6 @@
     hidden = gate_pre.shape[1]
     width, tall, quarter = features // replicas, rows // shards, rows // QUARTERS
     f32, bf16 = jnp.float32, jnp.bfloat16
-    vmem = pl.BlockSpec(memory_space=pltpu.VMEM)
     hbm = pl.BlockSpec(memory_space=pltpu.HBM)
     copies = 30
     return pl.pallas_call(
@@ -261,11 +279,16 @@
             jax.ShapeDtypeStruct((replicas * rows, hidden), bf16),
             jax.ShapeDtypeStruct((tall, features), f32),
             jax.ShapeDtypeStruct((rows, hidden), f32),
-            jax.ShapeDtypeStruct((8, 128), f32),
+            jax.ShapeDtypeStruct((8, hidden), f32),
         ),
         in_specs=[hbm] * 7,
-        out_specs=(vmem,) * 5,
+        out_specs=(hbm,) * 5,
         scratch_shapes=[
+            pltpu.VMEM((replicas * rows, width), bf16),
+            pltpu.VMEM((replicas * rows, hidden), bf16),
+            pltpu.VMEM((tall, features), f32),
+            pltpu.VMEM((rows, hidden), f32),
+            pltpu.VMEM((8, hidden), f32),
             pltpu.VMEM((rows, features), bf16),
             pltpu.VMEM((rows, hidden), bf16),
             pltpu.VMEM((rows, hidden), bf16),
@@ -285,11 +308,12 @@
             pltpu.VMEM((tall, features), f32),
             pltpu.VMEM((3, 8, 128), f32),
             pltpu.SemaphoreType.DMA((7,)),
+            pltpu.SemaphoreType.DMA((8,)),
             pltpu.SemaphoreType.DMA((copies,)),
             pltpu.SemaphoreType.DMA((copies,)),
         ],
         compiler_params=pltpu.CompilerParams(
-            collective_id=0, has_side_effects=True, vmem_limit_bytes=24 * 1024 * 1024
+            collective_id=0, has_side_effects=True, vmem_limit_bytes=54 * 1024 * 1024
         ),
         cost_estimate=pl.CostEstimate(
             flops=2 * rows * hidden * features, bytes_accessed=40 * 1024 * 1024, transcendentals=0
@@ -298,23 +322,103 @@
     )(inputs, gate_pre, up_pre, hidden_grad, segment_ids, doc_weight, w_gate)
 
 
+def step_kernel(
+    x_hbm, g_hbm, sum_hbm, up_hbm, gs_hbm, ma_old, mo_old, se_old,
+    ig_hbm, ug_hbm, ma_hbm, mo_hbm, se_hbm,
+    x_ref, g_ref, sum_ref, up_ref, gs_ref, ma_ref, mo_ref, se_ref, ig_v, ug_v, ma_v, mo_v, se_v, isem, sems,
+):
+    band = ma_v.shape[1]
+    written, loaded = [], []
+    bands = [pl.ds(k * band, band) for k in range(ma_v.shape[0])]
+    loads = [(g_hbm, g_ref), (x_hbm, x_ref), (gs_hbm, gs_ref)]
+    for at in bands:
+        loads += [
+            (old.at[at, :], new.at[at, :])
+            for old, new in ((mo_old, mo_ref), (se_old, se_ref), (ma_old, ma_ref))
+        ]
+    for k, (src, dst) in enumerate(loads + [(sum_hbm, sum_ref), (up_hbm, up_ref)]):
+        copy = pltpu.make_async_copy(src, dst, isem.at[k])
+        copy.start()
+        loaded.append(copy)
+
+    def write(src, dst):
+        copy = pltpu.make_async_copy(src, dst, sems.at[len(written)])
+        copy.start()
+        written.append(copy)
+
+    for copy in loaded[:3]:
+        copy.wait()
+    group_scale = gs_ref[0:1, :]
+    for k, at in enumerate(bands):
+        raw = lax.dot_general(
+            x_ref[:, at], g_ref[...], (((0,), (0,)), ((), ())), preferred_element_type=jnp.float32
+        )
+        grad = raw * group_scale
+        for copy in loaded[3 + 3 * k : 6 + 3 * k]:
+            copy.wait()
+        moment_new = 0.9 * mo_ref[at, :] + 0.1 * grad
+        second_new = 0.95 * se_ref[at, :] + 0.05 * grad * grad
+        mo_v[k] = moment_new
+        se_v[k] = second_new
+        master = ma_ref[at, :]
+        first_fix = moment_new * (1.0 / (1.0 - 0.9**8))
+        second_fix = second_new * (1.0 / (1.0 - 0.95**8))
+        ma_v[k] = master - 0.003 * (first_fix / (jnp.sqrt(second_fix) + 1e-08) + 0.1 * master)
+        write(mo_v.at[k], mo_hbm.at[at, :])
+        write(se_v.at[k], se_hbm.at[at, :])
+        write(ma_v.at[k], ma_hbm.at[at, :])
+    for copy in loaded[3 + 3 * len(bands) :]:
+        copy.wait()
+    ig_v[...] = sum_ref[...].astype(ig_v.dtype)
+    ug_v[...] = up_ref[...].astype(ug_v.dtype)
+    write(ig_v, ig_hbm)
+    write(ug_v, ug_hbm)
+    for copy in written:
+        copy.wait()
+
+
+def step(x_all, gate_all, input_scaled, up_scaled, group_scale, master, moment, second):
+    states = master.shape
+    bands = 4
+    f32, bf16 = jnp.float32, jnp.bfloat16
+    hbm = pl.BlockSpec(memory_space=pltpu.HBM)
+    banded = pltpu.VMEM((bands, states[0] // bands, states[1]), f32)
+    return pl.pallas_call(
+        step_kernel,
+        out_shape=(
+            jax.ShapeDtypeStruct(input_scaled.shape, bf16),
+            jax.ShapeDtypeStruct(up_scaled.shape, bf16),
+        )
+        + (jax.ShapeDtypeStruct(states, f32),) * 3,
+        in_specs=[hbm] * 8,
+        out_specs=(hbm,) * 5,
+        scratch_shapes=[
+            pltpu.VMEM(x_all.shape, bf16),
+            pltpu.VMEM(gate_all.shape, bf16),
+            pltpu.VMEM(input_scaled.shape, f32),
+            pltpu.VMEM(up_scaled.shape, f32),
+            pltpu.VMEM(group_scale.shape, f32),
+            pltpu.VMEM(states, f32),
+            pltpu.VMEM(states, f32),
+            pltpu.VMEM(states, f32),
+            pltpu.VMEM(input_scaled.shape, bf16),
+            pltpu.VMEM(up_scaled.shape, bf16),
+            banded,
+            banded,
+            banded,
+            pltpu.SemaphoreType.DMA((5 + 3 * bands,)),
+            pltpu.SemaphoreType.DMA((2 + 3 * bands,)),
+        ],
+        compiler_params=pltpu.CompilerParams(vmem_limit_bytes=54 * 1024 * 1024),
+        name="step",
+    )(x_all, gate_all, input_scaled, up_scaled, group_scale, master, moment, second)
+
+
 def gather_path(
     inputs, gate_pre, up_pre, hidden_grad, segment_ids, doc_weight, w_gate, master, moment, second
 ):
-    group_rows = inputs.shape[0]
-    replicas = lax.axis_size("replica")
-    x_all, gate_all, input_summed, up_part, totals = exchange(
-        inputs, gate_pre, up_pre, hidden_grad, segment_ids, doc_weight, w_gate
-    )
-    total = totals[0, 0]
-    scale = jnp.float32(group_rows * replicas) / total
-    group_scale = jnp.float32(group_rows) / total
-    input_grad = (input_summed * scale).astype(jnp.bfloat16)
-    up_grad = (up_part * scale).astype(jnp.bfloat16)
-    summed_grad = lax.dot_general(
-        x_all, gate_all, (((0,), (0,)), ((), ())), preferred_element_type=jnp.float32
-    )
-    return (input_grad, up_grad) + adamw(summed_grad * group_scale, master, moment, second)
+    factors = exchange(inputs, gate_pre, up_pre, hidden_grad, segment_ids, doc_weight, w_gate)
+    return step(*factors, master, moment, second)
 
 
 def on_device(*args):

time: 44.1 us -> 35.7 us (0.81)
  local copies, waits for them, and re-layouts: 7.9 us -> 0 us
  Pallas kernels: 27.5 us -> 35 us
  matrix products: 4.9 us -> 0 us
  between operations: 2.04 us -> 0.64 us
  other arithmetic: 1.38 us -> 0 us
    unnamed x20 -> x0, local copies, waits for them, and re-layouts: 7.39 us -> none
    pallas_call x0 -> x1, Pallas kernels: none -> 6.77 us  [step(): pl.pallas_call(step_kernel, out_shape=(jax.ShapeDtypeStruct(input_scaled....]
    dot_general x1 -> x0, matrix products: 4.9 us -> none  [gather_path(): lax.dot_general(x_all, gate_all, (((0,), (0,)), ((), ())), preferred_elem...]
    convert_element_type x2 -> x0, other arithmetic: 1.38 us -> none  [the longest x1 0.74 us: gather_path(): up_grad = (up_part * scale).astype(jnp.bfloat16)]
    pallas_call x1, Pallas kernels: 27.5 us -> 28.2 us  [exchange(): pl.pallas_call(exchange_kernel, out_shape=(jax.ShapeDtypeStruct((replicas...]
    slice x1 -> x0, local copies, waits for them, and re-layouts: 0.51 us -> none  [gather_path(): total = totals[0, 0]]
where the time goes in v2:
time: 35.7 us; the launch traced here: 35.6 us
  Pallas kernels  35 us (98%)
  between operations  0.64 us (2%)
    pallas_call x1, Pallas kernels, exchange(): pl.pallas_call(exchange_kernel, out_shape=(jax.ShapeDtypeStruct((replicas...  28.2 us
    pallas_call x1, Pallas kernels, step(): pl.pallas_call(step_kernel, out_shape=(jax.ShapeDtypeStruct(input_scaled....  6.77 us

profile of v2, /device:TPU:0, one launch (start us, length us, event | category | flops | bytes accessed | tf_op | source)
XLA Modules:
  0.0 35.6 jit_solution(535847099508921299)
XLA Ops:
  0.6 28.2 %exchange.1 = (bf16[512,512]{1,0:T(8,128)(2,1)}, bf16[512,1024]{1,0:T(8,128)(2,1)}, f32[16,2048]{1,0:T(8,128)}, f32[128,1024]{1,0:T(8,128)}, f32[8,1024]{1,0:T(8,128)}) custom-call(bf16[128,2048]{1,0:T(8,128)(2,1)} %x_hbm.1, bf16[128,1024]{1,0:T(8,128)(2,1)} %gate_hbm.1, bf16[128,1024]{1,0:T(8,128)(2,1)} %up_hbm.1, bf16[128,1024]{1,0:T(8,128)(2,1)} %hid_hbm.1, ...), custom_call_target="tpu_custom_call" | custom-call | flops 536870912 | bytes 41943040 | tf_op jit(solution)/shard_map/exchange/pallas_call | solution.py:275
  28.8 6.8 %step.1 = (bf16[16,2048]{1,0:T(8,128)(2,1)}, bf16[128,1024]{1,0:T(8,128)(2,1)}, f32[512,1024]{1,0:T(8,128)}, f32[512,1024]{1,0:T(8,128)}, f32[512,1024]{1,0:T(8,128)}) custom-call(bf16[512,512]{1,0:T(8,128)(2,1)} %get-tuple-element.10.x_hbm, bf16[512,1024]{1,0:T(8,128)(2,1)} %get-tuple-element.11.g_hbm, f32[16,2048]{1,0:T(8,128)} %get-tuple-element.12.sum_hbm, ...), custom_call_target="tpu_custom_call" | custom-call | tf_op jit(solution)/shard_map/step/pallas_call | solution.py:386

commit v3 on v2

--- a/solution.py
+++ b/solution.py
@@ -172,10 +172,13 @@
         return pl.ds(pl.multiple_of(index * tall, tall), tall)
 
     first = {}
-    for slot, (delta, index) in enumerate(
-        [(6, flip(flip(near, 2), 4)), (2, flip(near, 2)), (4, flip(near, 4)), (0, near)]
-    ):
+
+    def send_first(delta, index):
+        slot = len(first)
         first[delta] = (slot, push(part.at[block(index), :], rs1.at[slot], (r, near)))
+
+    send_first(6, flip(flip(near, 2), 4))
+    send_first(2, flip(near, 2))
 
     def absorb(delta, index):
         slot, copy = first[delta]
@@ -203,6 +206,8 @@
         copy.wait_recv()
         x_near.append(push(xq.at[group, 0], xq.at[group, 1], (r, near)))
         x_mid.append(push(xq.at[group, 0], xq.at[group, 2], (r, mid)))
+    send_first(4, flip(near, 4))
+    send_first(0, near)
     x_core.wait_recv()
     xo_ref[pl.ds(rows, rows), :] = xp[...].astype(bf16)
     g_core.wait_recv()
@@ -227,37 +232,37 @@
     absorb(2, mid)
     second_own = push(part.at[block(mid), :], rs2.at[1], (r, mid))
     g_across.append(relay_g(1))
-    absorb(4, far)
-    second_far.wait_recv()
-    part[block(far), :] = part[block(far), :] + rs2[0]
-    third = push(part.at[block(far), :], rs3, (r, far))
+    g_across.append(relay_g(2))
     x_last = []
     for group in range(2):
         x_near[group].wait_recv()
         x_last.append(push(xq.at[group, 1], xq.at[group, 3], (r, mid)))
         keep_x(group, 1, lax.rem(near, QUARTERS))
-    g_across.append(relay_g(2))
     for group in range(2):
         x_mid[group].wait_recv()
         keep_x(group, 2, lax.rem(mid, QUARTERS))
     for k in range(2):
         g_across[k].wait_recv()
         keep_g(2, k)
-    absorb(0, s)
-    second_own.wait_recv()
     g_across.append(relay_g(3))
+    write(go_ref.at[pl.ds(2 * rows, rows), :], go_hbm.at[pl.ds(2 * rows, rows), :])
+    absorb(4, far)
+    second_far.wait_recv()
+    part[block(far), :] = part[block(far), :] + rs2[0]
+    third = push(part.at[block(far), :], rs3, (r, far))
     for group in range(2):
         x_last[group].wait_recv()
         keep_x(group, 3, lax.rem(flip(near, 2), QUARTERS))
     write(xo_ref.at[pl.ds(2 * rows, 2 * rows), :], xo_hbm.at[pl.ds(2 * rows, 2 * rows), :])
-    write(go_ref.at[pl.ds(2 * rows, rows), :], go_hbm.at[pl.ds(2 * rows, rows), :])
-    third.wait_recv()
-    sum_ref[...] = (part[block(s), :] + rs2[1] + rs3[...]) * scale
-    write(sum_ref, sum_hbm)
     for k in range(2, QUARTERS):
         g_across[k].wait_recv()
         keep_g(2, k)
     write(go_ref.at[pl.ds(3 * rows, rows), :], go_hbm.at[pl.ds(3 * rows, rows), :])
+    absorb(0, s)
+    second_own.wait_recv()
+    third.wait_recv()
+    sum_ref[...] = (part[block(s), :] + rs2[1] + rs3[...]) * scale
+    write(sum_ref, sum_hbm)
     for copy in started:
         copy.wait_send()
     for copy in written:

time: 35.7 us -> 36.6 us (1.025)
  Pallas kernels: 35 us -> 35.8 us
    pallas_call x1, Pallas kernels: 28.2 us -> 29 us  [exchange(): pl.pallas_call(exchange_kernel, out_shape=(jax.ShapeDtypeStruct((replicas...]
where the time goes in v3:
time: 36.6 us; the launch traced here: 36.4 us
  Pallas kernels  35.8 us (98%)
  between operations  0.64 us (2%)
    pallas_call x1, Pallas kernels, exchange(): pl.pallas_call(exchange_kernel, out_shape=(jax.ShapeDtypeStruct((replicas...  29 us
    pallas_call x1, Pallas kernels, step(): pl.pallas_call(step_kernel, out_shape=(jax.ShapeDtypeStruct(input_scaled....  6.77 us

profile of v3, /device:TPU:0, one launch (start us, length us, event | category | flops | bytes accessed | tf_op | source)
XLA Modules:
  0.0 36.4 jit_solution(10508308403082157975)
XLA Ops:
  0.6 29.0 %exchange.1 = (bf16[512,512]{1,0:T(8,128)(2,1)}, bf16[512,1024]{1,0:T(8,128)(2,1)}, f32[16,2048]{1,0:T(8,128)}, f32[128,1024]{1,0:T(8,128)}, f32[8,1024]{1,0:T(8,128)}) custom-call(bf16[128,2048]{1,0:T(8,128)(2,1)} %x_hbm.1, bf16[128,1024]{1,0:T(8,128)(2,1)} %gate_hbm.1, bf16[128,1024]{1,0:T(8,128)(2,1)} %up_hbm.1, bf16[128,1024]{1,0:T(8,128)(2,1)} %hid_hbm.1, ...), custom_call_target="tpu_custom_call" | custom-call | flops 536870912 | bytes 41943040 | tf_op jit(solution)/shard_map/exchange/pallas_call | solution.py:280
  29.6 6.8 %step.1 = (bf16[16,2048]{1,0:T(8,128)(2,1)}, bf16[128,1024]{1,0:T(8,128)(2,1)}, f32[512,1024]{1,0:T(8,128)}, f32[512,1024]{1,0:T(8,128)}, f32[512,1024]{1,0:T(8,128)}) custom-call(bf16[512,512]{1,0:T(8,128)(2,1)} %get-tuple-element.10.x_hbm, bf16[512,1024]{1,0:T(8,128)(2,1)} %get-tuple-element.11.g_hbm, f32[16,2048]{1,0:T(8,128)} %get-tuple-element.12.sum_hbm, ...), custom_call_target="tpu_custom_call" | custom-call | tf_op jit(solution)/shard_map/step/pallas_call | solution.py:391
